TPU v7x, 512 devices: a whole 4x8x8 slice. The times are simulated.
512 devices in a mesh: fsdp: 64 (over y, x, z_lo), tp: 8 (over z_hi, core).
Axes of the slice: x: 4, y: 8, z: 8 (z_hi: 4, z_lo: 2; z = z_hi * 2 + z_lo), core: 2. Of those that a mesh axis runs over, the one named last changes fastest.
Arguments:
- saved_master: float32 [16384, 5120], P(('fsdp', 'tp')), may hold values from -6 to 6
- saved_first: float32 [16384, 5120], P(('fsdp', 'tp')), may hold values from -6 to 6
- saved_second: float32 [16384, 5120], P(('fsdp', 'tp')), may hold values from 0.05 to 20
- grad: bfloat16 [16384, 5120], P('fsdp', 'tp'), may hold values from -10000 to 10000
- row_target: int32 [16384], replicated, may hold values from 0 to 16383, as said below
- step: int32 [1], replicated, may hold values from 1 to 63
Outputs:
- new_master: float32 [16384, 5120], P('fsdp', 'tp')
- new_first: float32 [16384, 5120], P('fsdp', 'tp')
- new_second: float32 [16384, 5120], P('fsdp', 'tp')
- direction: float32 [16384, 5120], P('fsdp', 'tp')
Inputs may be any that keep to these rules, and one draw needn't show every extreme that they name: `row_target`: a permutation of 0 to 16383; the saved rows j * 256 to (j + 1) * 256 - 1 of every block j send exactly 4 rows into every new block of 256 rows.
All inputs are finite; a program needn't handle non-finite values.
Results may differ from a plain program's by a relative error of at most 0.0003.
Values sent between devices are 32-bit elements; how exact they have to be, the bound alone decides.
A program may use at most 64 MiB of HBM per device.

v0:
```python
import math

import jax
import jax.numpy as jnp
from jax import lax
from jax.sharding import PartitionSpec as P

H = 16384
D = 5120


beta_one = 0.9
beta_two = 0.95
epsilon = 1e-08
learn_rate = 0.001
weight_decay = 0.1


def sent_together(arrays, axis, split_dim, concat_dim, along):
    ends, at = ([], 0)
    for a in arrays[:-1]:
        at += a.shape[along]
        ends.append(at)
    both = jnp.concatenate(arrays, axis=along)
    return tuple(
        jnp.split(
            lax.all_to_all(both, axis, split_axis=split_dim, concat_axis=concat_dim, tiled=True),
            ends,
            axis=along,
        )
    )


def adam_update(master, first, second, grad, scale, step):
    clipped = scale * grad.astype(jnp.float32)
    first_new = beta_one * first + (1.0 - beta_one) * clipped
    second_new = beta_two * second + (1.0 - beta_two) * clipped * clipped
    count = step[0].astype(jnp.float32)
    first_hat = first_new / (1.0 - jnp.power(jnp.float32(beta_one), count))
    second_hat = second_new / (1.0 - jnp.power(jnp.float32(beta_two), count))
    direction = first_hat / (jnp.sqrt(second_hat) + epsilon) + weight_decay * master
    return (master - learn_rate * direction, first_new, second_new, direction)


def per_device(saved_master, saved_first, saved_second, grad, row_target, step):
    tp_count = lax.axis_size("tp")
    fsdp_count = lax.axis_size("fsdp")
    block_index = lax.axis_index("fsdp")
    block_rows = grad.shape[0]
    all_rows = row_target.shape[0]
    grad_wide = grad.astype(jnp.float32)
    local_square = jnp.sum(grad_wide * grad_wide)
    mine = lax.dynamic_slice_in_dim(row_target, block_index * block_rows, block_rows)
    send_order = jnp.argsort(mine, stable=True)
    positions = jnp.arange(all_rows, dtype=jnp.int32)
    in_block = row_target // block_rows == block_index
    sort_keys = jnp.where(
        in_block, positions // block_rows * all_rows + row_target, all_rows * all_rows
    )
    picked = jnp.argsort(sort_keys, stable=True)[:block_rows]
    arrived_rows = row_target[picked] - block_index * block_rows
    place_order = jnp.argsort(arrived_rows, stable=True)
    tp_copies = jnp.full((1, tp_count), local_square, jnp.float32)
    middle = (
        lax.all_to_all(saved_master, "tp", split_axis=1, concat_axis=0, tiled=True),
        lax.all_to_all(saved_first, "tp", split_axis=1, concat_axis=0, tiled=True),
        lax.all_to_all(saved_second, "tp", split_axis=1, concat_axis=0, tiled=True),
        lax.all_to_all(tp_copies, "tp", split_axis=1, concat_axis=0, tiled=True),
    )
    row_square = jnp.sum(middle[3])
    fsdp_copies = jnp.full((fsdp_count, 1), row_square, jnp.float32)
    arrived = (
        *sent_together(
            (middle[0][send_order], middle[1][send_order], middle[2][send_order]), "fsdp", 0, 0, 1
        ),
        lax.all_to_all(fsdp_copies, "fsdp", split_axis=0, concat_axis=0, tiled=True),
    )
    total = jnp.sum(arrived[3])
    master = arrived[0][place_order]
    first = arrived[1][place_order]
    second = arrived[2][place_order]
    scale = jnp.minimum(1.0, math.sqrt(H * D) / jnp.sqrt(total))
    return adam_update(master, first, second, grad, scale, step)


def solution(mesh):
    in_specs = (
        P(("fsdp", "tp"), None),
        P(("fsdp", "tp"), None),
        P(("fsdp", "tp"), None),
        P("fsdp", "tp"),
        P(),
        P(),
    )
    out_specs = (P("fsdp", "tp"), P("fsdp", "tp"), P("fsdp", "tp"), P("fsdp", "tp"))
    return jax.shard_map(
        per_device, mesh=mesh, in_specs=in_specs, out_specs=out_specs, check_vma=False
    )
```

profile of v0, /device:TPU:8, one launch (start us, length us, event | category | flops | bytes accessed | tf_op | source)
XLA Modules:
  0.0 176.6 jit_solution(5469844247020452423)
XLA Ops:
  0.6 0.0 copy-start.2
  0.6 1.8 %fusion.2 = f32[]{:T(128)} fusion(bf16[256,640]{1,0:T(8,128)(2,1)} %param.9), kind=kLoop, calls=%fused_computation.13 | loop fusion | flops 491519 | bytes 327684 | tf_op jit(solution)/shard_map/reduce_sum | solution.py:52
  2.5 1.2 broadcast_in_dim.27
  3.7 10.3 %all-to-all-start.4 = ((f32[1,8,1]{2,0,1:T(1,128)}), f32[1,8,1]{2,0,1:T(1,128)S(1)}, u32[]{:S(2)}, u32[]{:S(2)}) async-start(f32[1,8,1]{2,0,1:T(1,128)} %broadcast_in_dim.27), calls=%async_computation.4 | async-start | bytes 8192 | tf_op jit(solution)/shard_map/all_to_all | solution.py:68
  14.0 2.0 %copy.35 = f32[4,8,8,640]{3,2,0,1:T(8,128)} copy(f32[4,8,8,640]{3,2,1,0:T(8,128)} %bitcast.26) | data formatting | bytes 1310720 | tf_op jit(solution)/shard_map/all_to_all | solution.py:65
  16.0 5.7 %all-to-all-done.4 = f32[1,8,1]{2,0,1:T(1,128)S(1)} async-done(((f32[1,8,1]{2,0,1:T(1,128)}), f32[1,8,1]{2,0,1:T(1,128)S(1)}, u32[]{:S(2)}, u32[]{:S(2)}) %all-to-all-start.4) | async-done | bytes 64 | tf_op jit(solution)/shard_map/all_to_all | solution.py:68
  21.6 0.0 copy-start.3
  21.6 3.7 %all-to-all-start = ((f32[32,8,640]{2,0,1:T(8,128)}), f32[32,8,640]{2,0,1:T(8,128)S(1)}, u32[]{:S(2)}, u32[]{:S(2)}) async-start(f32[32,8,640]{2,0,1:T(8,128)} %bitcast.22), calls=%async_computation | async-start | bytes 1310720 | tf_op jit(solution)/shard_map/all_to_all | solution.py:65
  25.3 0.0 copy-done.2
  25.3 0.9 copy.34
  26.2 20.2 %all-to-all-done = f32[32,8,640]{2,0,1:T(8,128)S(1)} async-done(((f32[32,8,640]{2,0,1:T(8,128)}), f32[32,8,640]{2,0,1:T(8,128)S(1)}, u32[]{:S(2)}, u32[]{:S(2)}) %all-to-all-start) | async-done | bytes 655392 | tf_op jit(solution)/shard_map/all_to_all | solution.py:65
  46.4 0.0 copy-start
  46.4 3.7 %all-to-all-start.1 = ((f32[32,8,640]{2,0,1:T(8,128)}), f32[32,8,640]{2,0,1:T(8,128)S(1)}, u32[]{:S(2)}, u32[]{:S(2)}) async-start(f32[32,8,640]{2,0,1:T(8,128)} %bitcast.21), calls=%async_computation.1 | async-start | bytes 1310720 | tf_op jit(solution)/shard_map/all_to_all | solution.py:66
  50.1 0.0 copy-done.3
  50.1 0.9 copy.33
  51.0 19.5 %all-to-all-done.1 = f32[32,8,640]{2,0,1:T(8,128)S(1)} async-done(((f32[32,8,640]{2,0,1:T(8,128)}), f32[32,8,640]{2,0,1:T(8,128)S(1)}, u32[]{:S(2)}, u32[]{:S(2)}) %all-to-all-start.1) | async-done | bytes 655392 | tf_op jit(solution)/shard_map/all_to_all | solution.py:66
  70.5 3.5 %all-to-all-start.2 = ((f32[32,8,640]{2,0,1:T(8,128)}), f32[32,8,640]{2,0,1:T(8,128)S(1)}, u32[]{:S(2)}, u32[]{:S(2)}) async-start(f32[32,8,640]{2,0,1:T(8,128)} %bitcast.20), calls=%async_computation.2 | async-start | bytes 1310720 | tf_op jit(solution)/shard_map/all_to_all | solution.py:67
  74.0 0.0 copy-done
  74.0 0.1 dynamic_slice.3
  74.1 3.2 %sort.48 = (s32[256]{0:T(256)}, s32[256]{0:T(256)S(1)}) sort(s32[256]{0:T(256)S(1)} %dynamic_slice.3, s32[256]{0:T(256)S(1)} %iota.14), dimensions={0}, to_apply=%region_0.0 | sort | flops 2048 | bytes 4096 | tf_op jit(solution)/shard_map/jit(argsort)/sort | solution.py:54
  77.3 0.6 reduce_sum.28
  77.9 1.1 gather_fusion
  79.0 1.1 gather_fusion.1
  80.1 12.7 %all-to-all-done.2 = f32[32,8,640]{2,0,1:T(8,128)S(1)} async-done(((f32[32,8,640]{2,0,1:T(8,128)}), f32[32,8,640]{2,0,1:T(8,128)S(1)}, u32[]{:S(2)}, u32[]{:S(2)}) %all-to-all-start.2) | async-done | bytes 655392 | tf_op jit(solution)/shard_map/all_to_all | solution.py:67
  92.8 1.3 broadcast_in_dim.28
  94.1 12.0 %all-to-all-start.5 = ((f32[64,1,1]{2,1,0:T(1,128)}), f32[64,1,1]{2,1,0:T(1,128)S(1)}, u32[]{:S(2)}, u32[]{:S(2)}) async-start(f32[64,1,1]{2,1,0:T(1,128)} %broadcast_in_dim.28), calls=%async_computation.5 | async-start | bytes 65536 | tf_op jit(solution)/shard_map/all_to_all | solution.py:76
  106.1 1.9 %gather_fusion.2 = f32[256,640]{1,0:T(8,128)} fusion(f32[256,640]{1,0:T(8,128)S(1)} %bitcast.24, s32[1024]{0:T(1024)S(1)} %pad_clamp_fusion.2), kind=kCustom, calls=%fused_computation.2 | custom fusion | bytes 1311744 | tf_op jit(solution)/shard_map/gather | solution.py:74
  108.0 1.2 pad_maximum_fusion
  109.2 1.9 %all_to_all.74 = f32[64,4,1920]{2,1,0:T(4,128)} reshape(f32[256,1920]{1,0:T(8,128)S(1)} %pad_maximum_fusion) | data formatting | bytes 3932160 | tf_op jit(solution)/shard_map/all_to_all | solution.py:27
  111.1 4.4 %all-to-all-done.5 = f32[64,1,1]{2,1,0:T(1,128)S(1)} async-done(((f32[64,1,1]{2,1,0:T(1,128)}), f32[64,1,1]{2,1,0:T(1,128)S(1)}, u32[]{:S(2)}, u32[]{:S(2)}) %all-to-all-start.5) | async-done | bytes 288 | tf_op jit(solution)/shard_map/all_to_all | solution.py:76
  115.5 6.8 %all-to-all-start.3 = ((f32[64,4,1920]{2,1,0:T(4,128)}), f32[64,4,1920]{2,1,0:T(4,128)S(1)}, u32[]{:S(2)}, u32[]{:S(2)}) async-start(f32[64,4,1920]{2,1,0:T(4,128)} %all_to_all.74), calls=%async_computation.3 | async-start | bytes 3932160 | tf_op jit(solution)/shard_map/all_to_all | solution.py:27
  122.3 0.1 fusion.8
  122.4 7.8 %sort.49 = (s32[16384]{0:T(1024)}, s32[16384]{0:T(1024)S(1)}) sort(s32[16384]{0:T(1024)S(1)} %fusion.8, s32[16384]{0:T(1024)S(1)} %iota.16), dimensions={0}, to_apply=%region_1.0 | sort | flops 229376 | bytes 262144 | tf_op jit(solution)/shard_map/jit(argsort)/sort | solution.py:60
  130.1 1.7 gather_fusion.3
  132.6 3.2 %sort.50 = (s32[256]{0:T(256)}, s32[256]{0:T(256)S(1)}) sort(s32[256]{0:T(256)S(1)} %broadcast_subtract_fusion, s32[256]{0:T(256)S(1)} %iota.17), dimensions={0}, to_apply=%region_2.3 | sort | flops 2048 | bytes 4096 | tf_op jit(solution)/shard_map/jit(argsort)/sort | solution.py:62
  135.8 0.7 reduce_sum.29
  137.2 30.8 %all-to-all-done.3 = f32[64,4,1920]{2,1,0:T(4,128)S(1)} async-done(((f32[64,4,1920]{2,1,0:T(4,128)}), f32[64,4,1920]{2,1,0:T(4,128)S(1)}, u32[]{:S(2)}, u32[]{:S(2)}) %all-to-all-start.3) | async-done | bytes 1966112 | tf_op jit(solution)/shard_map/all_to_all | solution.py:27
  167.9 2.0 %all_to_all.76 = f32[256,1920]{1,0:T(8,128)} reshape(f32[64,4,1920]{2,1,0:T(4,128)S(1)} %all-to-all-done.3) | data formatting | bytes 3932160 | tf_op jit(solution)/shard_map/all_to_all | solution.py:27
  169.9 1.6 fusion.15
  171.5 1.1 gather_fusion.5
  172.6 1.1 gather_fusion.6
  173.7 0.0 copy-start.1
  173.7 1.1 gather_fusion.4
  174.8 0.0 copy-done.1
  174.8 1.8 %multiply_subtract_fusion = (f32[256,640]{1,0:T(8,128)}, f32[256,640]{1,0:T(8,128)}, f32[256,640]{1,0:T(8,128)}, f32[256,640]{1,0:T(8,128)}) fusion(f32[256,640]{1,0:T(8,128)S(1)} %gather_fusion.4, f32[]{:T(128)} %bitcast.7, f32[]{:T(128)} %bitcast.6, bf16[256,640]{1,0:T(8,128)(2,1)S(1)} %copy-done.1, f32[]{:T(128)S(6)} %min.3, ...), kind=kLoop, calls=%fused_computation.18 | loop fusion | flops 2785280 | bytes 4915212 | tf_op jit(solution)/shard_map/sub | solution.py:42
  (10 shorter events, 0.1 us)
Async XLA Ops:
  0.6 24.7 %copy-start.2 = (f32[32,5120]{1,0:T(8,128)S(1)}, f32[32,5120]{1,0:T(8,128)}, u32[]{:S(2)}) copy-start(f32[32,5120]{1,0:T(8,128)} %param.7) | copy-start | bytes 1966084
  3.7 17.9 %all-to-all-start.4 = ((f32[1,8,1]{2,0,1:T(1,128)}), f32[1,8,1]{2,0,1:T(1,128)S(1)}, u32[]{:S(2)}, u32[]{:S(2)}) async-start(f32[1,8,1]{2,0,1:T(1,128)} %broadcast_in_dim.27), calls=%async_computation.4 | async-start | bytes 8192 | tf_op jit(solution)/shard_map/all_to_all | solution.py:68
  21.6 28.4 %copy-start.3 = (f32[32,5120]{1,0:T(8,128)S(1)}, f32[32,5120]{1,0:T(8,128)}, u32[]{:S(2)}) copy-start(f32[32,5120]{1,0:T(8,128)} %param.8) | copy-start | bytes 1966084
  21.6 24.8 %all-to-all-start = ((f32[32,8,640]{2,0,1:T(8,128)}), f32[32,8,640]{2,0,1:T(8,128)S(1)}, u32[]{:S(2)}, u32[]{:S(2)}) async-start(f32[32,8,640]{2,0,1:T(8,128)} %bitcast.22), calls=%async_computation | async-start | bytes 1310720 | tf_op jit(solution)/shard_map/all_to_all | solution.py:65
  46.4 27.6 %copy-start = (s32[16384]{0:T(1024)S(1)}, s32[16384]{0:T(1024)}, u32[]{:S(2)}) copy-start(s32[16384]{0:T(1024)} %param.10) | copy-start | bytes 196612
  46.4 24.1 %all-to-all-start.1 = ((f32[32,8,640]{2,0,1:T(8,128)}), f32[32,8,640]{2,0,1:T(8,128)S(1)}, u32[]{:S(2)}, u32[]{:S(2)}) async-start(f32[32,8,640]{2,0,1:T(8,128)} %bitcast.21), calls=%async_computation.1 | async-start | bytes 1310720 | tf_op jit(solution)/shard_map/all_to_all | solution.py:66
  70.5 22.3 %all-to-all-start.2 = ((f32[32,8,640]{2,0,1:T(8,128)}), f32[32,8,640]{2,0,1:T(8,128)S(1)}, u32[]{:S(2)}, u32[]{:S(2)}) async-start(f32[32,8,640]{2,0,1:T(8,128)} %bitcast.20), calls=%async_computation.2 | async-start | bytes 1310720 | tf_op jit(solution)/shard_map/all_to_all | solution.py:67
  94.1 21.4 %all-to-all-start.5 = ((f32[64,1,1]{2,1,0:T(1,128)}), f32[64,1,1]{2,1,0:T(1,128)S(1)}, u32[]{:S(2)}, u32[]{:S(2)}) async-start(f32[64,1,1]{2,1,0:T(1,128)} %broadcast_in_dim.28), calls=%async_computation.5 | async-start | bytes 65536 | tf_op jit(solution)/shard_map/all_to_all | solution.py:76
  115.5 52.4 %all-to-all-start.3 = ((f32[64,4,1920]{2,1,0:T(4,128)}), f32[64,4,1920]{2,1,0:T(4,128)S(1)}, u32[]{:S(2)}, u32[]{:S(2)}) async-start(f32[64,4,1920]{2,1,0:T(4,128)} %all_to_all.74), calls=%async_computation.3 | async-start | bytes 3932160 | tf_op jit(solution)/shard_map/all_to_all | solution.py:27
  173.7 1.1 copy-start.1
where the time goes:
time: 177 us
  waiting for transfers between devices  93.3 us (53%)
  starting transfers between devices  39.9 us (23%)
  local copies, waits for them, and re-layouts  20.9 us (12%)
  other arithmetic  20.3 us (11%)
  between operations  2.23 us (1%)
    all_to_all x1, waiting for transfers between devices, sent_together(): lax.all_to_all(both, axis, split_axis=split_dim, concat_axis=concat_dim,...  30.8 us
    all_to_all x1, waiting for transfers between devices, per_device(): lax.all_to_all(saved_master, 'tp', split_axis=1, concat_axis=0, tiled=True)  20.2 us
    all_to_all x1, waiting for transfers between devices, per_device(): lax.all_to_all(saved_first, 'tp', split_axis=1, concat_axis=0, tiled=True)  19.5 us
    all_to_all x1, waiting for transfers between devices, per_device(): lax.all_to_all(saved_second, 'tp', split_axis=1, concat_axis=0, tiled=True)  12.7 us
    all_to_all x1, starting transfers between devices, per_device(): lax.all_to_all(fsdp_copies, 'fsdp', split_axis=0, concat_axis=0, tiled=True)  12 us
    all_to_all x1, starting transfers between devices, per_device(): lax.all_to_all(tp_copies, 'tp', split_axis=1, concat_axis=0, tiled=True)  10.3 us
    sort x1, other arithmetic, per_device(): picked = jnp.argsort(sort_keys, stable=True)[:block_rows]  7.75 us
    all_to_all x1, starting transfers between devices, sent_together(): lax.all_to_all(both, axis, split_axis=split_dim, concat_axis=concat_dim,...  6.77 us
  transfers between devices with their start and end apart: 6, of which 6 were waited for; matrix products, arithmetic and copies ran while one was open for 15% of the time, Pallas kernels for 0%

commit v1 on v0

v1 whole, which is shorter than its diff:
```python
import functools
import math

import jax
import jax.numpy as jnp
from jax import lax
from jax.experimental import pallas as pl
from jax.experimental.pallas import tpu as pltpu
from jax.sharding import PartitionSpec as P

H = 16384
D = 5120
F = 64
T = 8
N_Y, N_X, N_Z = 8, 4, 2
ROWS = H // F
PIECE = ROWS // T
COLS = D // T
LANES = 128
PER = COLS // LANES
BLOCKS = 3 * PER
UNITS = (BLOCKS + 1) // 2
SLOTS = 8 * F

beta_one = 0.9
beta_two = 0.95
epsilon = 1e-08
learn_rate = 0.001
weight_decay = 0.1

MESH = pl.DeviceIdType.MESH
F32, BF16, I32 = jnp.float32, jnp.bfloat16, jnp.int32


def two_parts(x):
    high = x.astype(BF16)
    low = (x - high.astype(F32)).astype(BF16)
    return jnp.concatenate([high, low], axis=1)


def moved(order, x):
    both = jnp.dot(order, two_parts(x), preferred_element_type=F32)
    return both[:, :LANES] + both[:, LANES:]


def fsdp_peer(me, i):
    y, x, z = me // (N_X * N_Z), me // N_Z % N_X, me % N_Z
    y = (y + i // (N_X * N_Z)) % N_Y
    x = (x + i // N_Z % N_X) % N_X
    z = (z + i % N_Z) % N_Z
    return (y * N_X + x) * N_Z + z


def tp_peer(me, i):
    return (me // 2 + i // 2) % 4 * 2 + (me + i) % 2


def kernel(
    master, first, second, grad, targets, out, total,
    whole, leaving, arrived, sums_out, sums, wide, to_slot, to_row,
    own_sem, sum_sem, tp_sem, fsdp_sem, sum_sent, tp_sent, fsdp_sent,
):
    f, t = lax.axis_index("fsdp"), lax.axis_index("tp")
    barrier = pltpu.get_barrier_semaphore()

    def greet_tp(i, carry):
        pl.semaphore_signal(barrier, inc=1, device_id=(f, tp_peer(t, i)), device_id_type=MESH)
        return carry

    def greet_fsdp(i, carry):
        pl.semaphore_signal(barrier, inc=1, device_id=(fsdp_peer(f, i), t), device_id_type=MESH)
        return carry

    lax.fori_loop(1, T, greet_tp, 0)
    lax.fori_loop(1, F, greet_fsdp, 0)

    saved = (master, first, second)
    here = pl.ds(pl.multiple_of(t * PIECE, PIECE), PIECE)
    own = []
    for b in range(BLOCKS):
        a, c = divmod(b, PER)
        at = pl.multiple_of(t * COLS + c * LANES, LANES)
        copy = pltpu.make_async_copy(saved[a].at[:, pl.ds(at, LANES)], whole.at[b, here, :], own_sem.at[b])
        copy.start()
        own.append(copy)

    square = jnp.zeros((8, LANES), F32)
    for c in range(PER):
        wide_grad = grad[:, c * LANES : (c + 1) * LANES].astype(F32)
        square += jnp.sum((wide_grad * wide_grad).reshape(ROWS // 8, 8, LANES), axis=0)
    sums_out[...] = square
    mine_sum = pl.ds(pl.multiple_of(t * 8, 8), 8)
    sums[mine_sum, :] = square

    pl.semaphore_wait(barrier, F + T - 2)

    def send_sum(i, carry):
        pltpu.make_async_remote_copy(
            src_ref=sums_out, dst_ref=sums.at[mine_sum, :], send_sem=sum_sent, recv_sem=sum_sem,
            device_id=(f, tp_peer(t, i)), device_id_type=MESH,
        ).start()
        return carry

    for b in range(BLOCKS):
        a, c = divmod(b, PER)

        def send_piece(i, carry, a=a, b=b, c=c):
            other = tp_peer(t, i)
            at = pl.multiple_of(other * COLS + c * LANES, LANES)
            pltpu.make_async_remote_copy(
                src_ref=saved[a].at[:, pl.ds(at, LANES)], dst_ref=whole.at[b, here, :],
                send_sem=tp_sent, recv_sem=tp_sem.at[b],
                device_id=(f, other), device_id_type=MESH,
            ).start()
            return carry

        lax.fori_loop(1, T, send_piece, 0)
        if b == 1:
            lax.fori_loop(1, T, send_sum, 0)

    mine = jnp.concatenate([targets[pl.ds(2 * f, 1), :], targets[pl.ds(2 * f + 1, 1), :]], axis=1).astype(F32)
    across = jnp.broadcast_to(mine, (ROWS, ROWS))
    slot = jnp.sum(jnp.where(across.T < across, 1.0, 0.0), axis=0, keepdims=True)
    line = lax.broadcasted_iota(I32, (SLOTS, 2 * ROWS), 0)
    lane = lax.broadcasted_iota(I32, (SLOTS, 2 * ROWS), 1)
    line_key = line // 8 * 4 + line % 4 + line // 4 % 2 * 1024
    slot_key = jnp.concatenate([slot, slot + 1024.0], axis=1)
    to_slot[...] = jnp.where(line_key.astype(F32) == slot_key, 1.0, 0.0).astype(BF16)

    def widen(s, carry):
        at = pl.ds(pl.multiple_of(8 * s, 8), 8)
        wide[at, :LANES] = jnp.broadcast_to(targets[pl.ds(2 * s, 1), :], (8, LANES))
        wide[at, LANES:] = jnp.broadcast_to(targets[pl.ds(2 * s + 1, 1), :], (8, LANES))
        return carry

    lax.fori_loop(0, F, widen, 0)
    left = jnp.where(wide[...] // ROWS == f, wide[...] % ROWS, 4096).astype(F32)
    nth = lax.broadcasted_iota(I32, (SLOTS, 1), 0)
    row = jnp.zeros((SLOTS, 1), F32)
    for n in range(4):
        least = jnp.min(left, axis=1, keepdims=True)
        row = jnp.where(nth % 4 == n, least, row)
        if n < 3:
            left = jnp.where(left == least, 4096.0, left)
    row_key = row + (nth // 4 % 2 * 1024).astype(F32)
    lane_key = (lane % ROWS + lane // ROWS * 1024).astype(F32)
    to_row[...] = jnp.where(row_key == lane_key, 1.0, 0.0).T.astype(BF16)

    for copy in own:
        copy.wait()
    pltpu.make_async_copy(sums.at[pl.ds(0, 8 * (T - 1)), :], sums.at[pl.ds(0, 8 * (T - 1)), :], sum_sem).wait()
    whole[BLOCKS, :, :] = jnp.broadcast_to(jnp.sum(sums[...], axis=0, keepdims=True), (ROWS, LANES))

    others = ROWS - PIECE
    to_me = pl.ds(pl.multiple_of(8 * f, 8), 8)

    def send_unit(u, carry):
        def arrive(b):
            part = whole.at[b, pl.ds(0, others), :]
            pltpu.make_async_copy(part, part, tp_sem.at[b]).wait()

        arrive(2 * u)

        @pl.when(2 * u + 1 < BLOCKS)
        def _():
            arrive(2 * u + 1)

        both = jnp.concatenate([whole[2 * u], whole[2 * u + 1]], axis=0)
        leaving[u] = moved(to_slot[...], both)
        arrived[u, to_me, :] = leaving[u, to_me, :]

        def send(i, carry):
            other = fsdp_peer(f, i)
            pltpu.make_async_remote_copy(
                src_ref=leaving.at[u, pl.ds(pl.multiple_of(8 * other, 8), 8), :],
                dst_ref=arrived.at[u, to_me, :],
                send_sem=fsdp_sent, recv_sem=fsdp_sem.at[u],
                device_id=(other, t), device_id_type=MESH,
            ).start()
            return carry

        lax.fori_loop(1, F, send, 0)
        return carry

    lax.fori_loop(0, UNITS, send_unit, 0)

    def place_unit(u, carry):
        part = arrived.at[u, pl.ds(0, SLOTS - 8), :]
        pltpu.make_async_copy(part, part, fsdp_sem.at[u]).wait()
        both = moved(to_row[...], arrived[u])

        def put(b, value):
            out[b // PER, :, pl.ds(pl.multiple_of(b % PER * LANES, LANES), LANES)] = value

        put(2 * u, both[:ROWS])

        @pl.when(2 * u + 1 < BLOCKS)
        def _():
            put(2 * u + 1, both[ROWS:])

        @pl.when(2 * u + 1 == BLOCKS)
        def _():
            total[...] = jnp.broadcast_to(0.25 * jnp.sum(both[ROWS:]), (8, LANES))

        return carry

    lax.fori_loop(0, UNITS, place_unit, 0)

    pltpu.make_async_copy(sums.at[pl.ds(0, 8 * (T - 1)), :], sums.at[pl.ds(0, 8 * (T - 1)), :], sum_sent).wait()
    sent = whole.at[pl.ds(0, BLOCKS), pl.ds(0, others), :]
    pltpu.make_async_copy(sent, sent, tp_sent).wait()
    sent = leaving.at[:, pl.ds(0, SLOTS - 8), :]
    pltpu.make_async_copy(sent, sent, fsdp_sent).wait()


def restore(saved_master, saved_first, saved_second, grad, targets):
    vmem = pl.BlockSpec(memory_space=pltpu.VMEM)
    anywhere = pl.BlockSpec(memory_space=pl.ANY)
    dma = pltpu.SemaphoreType.DMA
    return pl.pallas_call(
        kernel,
        out_shape=(
            jax.ShapeDtypeStruct((3, ROWS, COLS), F32),
            jax.ShapeDtypeStruct((8, LANES), F32),
        ),
        in_specs=[anywhere, anywhere, anywhere, vmem, vmem],
        out_specs=(vmem, vmem),
        scratch_shapes=[
            pltpu.VMEM((BLOCKS + 1, ROWS, LANES), F32),
            pltpu.VMEM((UNITS, SLOTS, LANES), F32),
            pltpu.VMEM((UNITS, SLOTS, LANES), F32),
            pltpu.VMEM((8, LANES), F32),
            pltpu.VMEM((8 * T, LANES), F32),
            pltpu.VMEM((SLOTS, 2 * LANES), I32),
            pltpu.VMEM((SLOTS, SLOTS), BF16),
            pltpu.VMEM((SLOTS, SLOTS), BF16),
            dma((BLOCKS,)),
            dma,
            dma((BLOCKS,)),
            dma((UNITS,)),
            dma,
            dma,
            dma,
        ],
        name="restore",
        compiler_params=pltpu.CompilerParams(
            collective_id=0, has_side_effects=True, vmem_limit_bytes=48 * 1024 * 1024
        ),
    )(saved_master, saved_first, saved_second, grad, targets)


def adam_update(master, first, second, grad, scale, step):
    clipped = scale * grad.astype(jnp.float32)
    first_new = beta_one * first + (1.0 - beta_one) * clipped
    second_new = beta_two * second + (1.0 - beta_two) * clipped * clipped
    count = step[0].astype(jnp.float32)
    first_hat = first_new / (1.0 - jnp.power(jnp.float32(beta_one), count))
    second_hat = second_new / (1.0 - jnp.power(jnp.float32(beta_two), count))
    direction = first_hat / (jnp.sqrt(second_hat) + epsilon) + weight_decay * master
    return (master - learn_rate * direction, first_new, second_new, direction)


def per_device(saved_master, saved_first, saved_second, grad, row_target, step):
    targets = row_target.reshape(H // LANES, LANES)
    state, total = restore(saved_master, saved_first, saved_second, grad, targets)
    scale = jnp.minimum(1.0, math.sqrt(H * D) / jnp.sqrt(total[0, 0]))
    return adam_update(state[0], state[1], state[2], grad, scale, step)


def solution(mesh):
    in_specs = (
        P(("fsdp", "tp"), None),
        P(("fsdp", "tp"), None),
        P(("fsdp", "tp"), None),
        P("fsdp", "tp"),
        P(),
        P(),
    )
    out_specs = (P("fsdp", "tp"), P("fsdp", "tp"), P("fsdp", "tp"), P("fsdp", "tp"))
    return jax.shard_map(
        per_device, mesh=mesh, in_specs=in_specs, out_specs=out_specs, check_vma=False
    )
```

time: 177 us -> 106 us (0.60)
  the two profiles are of different devices: /device:TPU:8 before, /device:TPU:1 now
where the time goes in v1:
time: 106 us; the launch traced here: 105 us
  Pallas kernels  95.7 us (90%)
  local copies, waits for them, and re-layouts  5.58 us (5%)
  between operations  2.08 us (2%)
  other arithmetic  1.81 us (2%)
    pallas_call x1, Pallas kernels, restore(): pl.pallas_call(kernel, out_shape=(jax.ShapeDtypeStruct((3, ROWS, COLS), F...  95.7 us
    unnamed x10, local copies, waits for them, and re-layouts  5.07 us

profile of v1, /device:TPU:1, one launch (start us, length us, event | category | flops | bytes accessed | tf_op | source)
XLA Modules:
  0.0 105.2 jit_solution(9207426377157319449)
XLA Ops:
  1.4 0.0 copy-start
  1.4 1.0 copy-done
  2.3 0.0 copy-start.1
  2.3 1.1 %copy-done.1 = f32[32,5120]{1,0:T(8,128)S(1)} copy-done((f32[32,5120]{1,0:T(8,128)S(1)}, f32[32,5120]{1,0:T(8,128)}, u32[]{:S(2)}) %copy-start.1) | copy-done | bytes 655384
  3.4 0.0 copy-start.2
  3.4 1.1 %copy-done.2 = f32[32,5120]{1,0:T(8,128)S(1)} copy-done((f32[32,5120]{1,0:T(8,128)S(1)}, f32[32,5120]{1,0:T(8,128)}, u32[]{:S(2)}) %copy-start.2) | copy-done | bytes 655384
  4.5 0.0 copy-start.3
  4.5 1.1 %copy-done.3 = f32[32,5120]{1,0:T(8,128)S(1)} copy-done((f32[32,5120]{1,0:T(8,128)S(1)}, f32[32,5120]{1,0:T(8,128)}, u32[]{:S(2)}) %copy-start.3) | copy-done | bytes 655384
  5.6 0.0 copy-start.4
  5.6 0.8 copy-done.4
  6.4 95.7 %restore.1 = (f32[3,256,640]{2,1,0:T(8,128)S(1)}, f32[8,128]{1,0:T(8,128)S(1)}) custom-call(f32[32,5120]{1,0:T(8,128)S(1)} %copy-done.1, f32[32,5120]{1,0:T(8,128)S(1)} %copy-done.2, f32[32,5120]{1,0:T(8,128)S(1)} %copy-done.3, bf16[256,640]{1,0:T(8,128)(2,1)S(1)} %copy-done, s32[128,128]{1,0:T(8,128)S(1)} %bitcast.16), custom_call_target="tpu_custom_call" | custom-call | tf_op jit(solution)/shard_map/restore/pallas_call | solution.py:220
  102.1 0.5 slice.14
  103.3 1.8 %bitcast_subtract_fusion = (f32[256,640]{1,0:T(8,128)}, f32[256,640]{1,0:T(8,128)}, f32[256,640]{1,0:T(8,128)}, f32[256,640]{1,0:T(8,128)}) fusion(f32[3,256,640]{2,1,0:T(8,128)S(1)} %get-tuple-element.6, f32[]{:T(128)} %bitcast.6, f32[]{:T(128)} %bitcast.4, bf16[256,640]{1,0:T(8,128)(2,1)S(1)} %copy-done, f32[]{:T(128)} %bitcast.3), kind=kLoop, calls=%fused_computation.3 | loop fusion | flops 2785280 | bytes 4915212 | tf_op jit(solution)/shard_map/sub | solution.py:260
Async XLA Ops:
  1.4 1.0 copy-start
  2.3 1.1 %copy-start.1 = (f32[32,5120]{1,0:T(8,128)S(1)}, f32[32,5120]{1,0:T(8,128)}, u32[]{:S(2)}) copy-start(f32[32,5120]{1,0:T(8,128)} %master.1) | copy-start | bytes 1966084
  3.4 1.1 %copy-start.2 = (f32[32,5120]{1,0:T(8,128)S(1)}, f32[32,5120]{1,0:T(8,128)}, u32[]{:S(2)}) copy-start(f32[32,5120]{1,0:T(8,128)} %first.1) | copy-start | bytes 1966084
  4.5 1.1 %copy-start.3 = (f32[32,5120]{1,0:T(8,128)S(1)}, f32[32,5120]{1,0:T(8,128)}, u32[]{:S(2)}) copy-start(f32[32,5120]{1,0:T(8,128)} %second.1) | copy-start | bytes 1966084
  5.6 0.8 copy-start.4

commit v2 on v0

v2 whole, which is shorter than its diff:
```python
import functools
import math

import jax
import jax.numpy as jnp
from jax import lax
from jax.experimental import pallas as pl
from jax.experimental.pallas import tpu as pltpu
from jax.sharding import PartitionSpec as P

H = 16384
D = 5120
F = 64
T = 8
N_Y, N_X, N_Z = 8, 4, 2
ROWS = H // F
PIECE = ROWS // T
COLS = D // T
LANES = 128
PER = COLS // LANES
BLOCKS = 3 * PER + 1
SLOTS = 8 * F
LIMIT = math.sqrt(H * D)

beta_one = 0.9
beta_two = 0.95
epsilon = 1e-08
learn_rate = 0.001
weight_decay = 0.1

MESH = pl.DeviceIdType.MESH
F32, BF16, I32 = jnp.float32, jnp.bfloat16, jnp.int32
scope = jax.named_scope


def two_parts(x):
    high = x.astype(BF16)
    low = (x - high.astype(F32)).astype(BF16)
    return jnp.concatenate([high, low], axis=1)


def moved(order, x):
    both = jnp.dot(order, two_parts(x), preferred_element_type=F32)
    return both[:, :LANES] + both[:, LANES:]


def fsdp_peer(me, dy, dx, dz):
    y, x, z = me // (N_X * N_Z), me // N_Z % N_X, me % N_Z
    return ((y + dy) % N_Y * N_X + (x + dx) % N_X) * N_Z + (z + dz) % N_Z


def tp_peer(me, i):
    return (me // 2 + i // 2) % 4 * 2 + (me + i) % 2


def kernel(
    master, first, second, grad_in, targets_in, out, clipped,
    stage, grad, targets, whole, leaving, arrived, sums_out, sums, row_sum, row_sums, wide, to_slot, to_row,
    local_sem, own_sem, sum_sem, tp_sem, row_sem, fsdp_sem, sum_sent, tp_sent, row_sent, fsdp_sent, x_sem, z_sem,
):
    f, t = lax.axis_index("fsdp"), lax.axis_index("tp")
    barrier = pltpu.get_barrier_semaphore()

    def signal(semaphore, at):
        pl.semaphore_signal(semaphore, inc=1, device_id=at, device_id_type=MESH)

    arrived[0] = jnp.zeros((SLOTS, LANES), F32)
    row_sums[...] = jnp.zeros((SLOTS, LANES), F32)
    with scope("greet"):
        for dz in range(1, N_Z):
            signal(barrier, (fsdp_peer(f, 0, 0, dz), t))
        for dx in range(1, N_X):
            signal(barrier, (fsdp_peer(f, 0, dx, 0), t))
        for i in range(1, T):
            signal(barrier, (f, tp_peer(t, i)))
        for dy in range(1, N_Y):
            signal(barrier, (fsdp_peer(f, dy, 0, 0), t))

    with scope("local"):
        saved = (master, first, second)
        here = pl.ds(pl.multiple_of(t * PIECE, PIECE), PIECE)
        loads = []
        for a in range(3):
            copy = pltpu.make_async_copy(saved[a], stage.at[a], local_sem.at[a])
            copy.start()
            loads.append(copy)
        grad_load = pltpu.make_async_copy(grad_in, grad, local_sem.at[3])
        grad_load.start()
        target_load = pltpu.make_async_copy(targets_in, targets, local_sem.at[4])
        target_load.start()
        own = []
        for b in range(1, BLOCKS):
            a, c = divmod(b - 1, PER)
            at = pl.multiple_of(t * COLS + c * LANES, LANES)
            copy = pltpu.make_async_copy(saved[a].at[:, pl.ds(at, LANES)], whole.at[b, here, :], own_sem.at[b])
            copy.start()
            own.append(copy)
        loads[0].wait()

    with scope("barrier"):
        pl.semaphore_wait(barrier, (N_Y - 1) + (N_X - 1) + (N_Z - 1) + (T - 1))

    def send_block(b):
        a, c = (b - 1) // PER, (b - 1) % PER
        for i in range(1, T):
            other = tp_peer(t, i)
            at = pl.multiple_of(other * COLS + c * LANES, LANES)
            pltpu.make_async_remote_copy(
                src_ref=stage.at[a, :, pl.ds(at, LANES)], dst_ref=whole.at[b, here, :],
                send_sem=tp_sent, recv_sem=tp_sem.at[b],
                device_id=(f, other), device_id_type=MESH,
            ).start()

    with scope("issueA0"):
        send_block(1)
        for dx in range(1, N_X):
            signal(x_sem, (fsdp_peer(f, 0, dx, 0), t))
        grad_load.wait()
        square = jnp.zeros((8, LANES), F32)
        for c in range(PER):
            wide_grad = grad[:, c * LANES : (c + 1) * LANES].astype(F32)
            square += jnp.sum((wide_grad * wide_grad).reshape(ROWS // 8, 8, LANES), axis=0)
        sums_out[...] = square
        mine_sum = pl.ds(pl.multiple_of(t * 8, 8), 8)
        sums[mine_sum, :] = square
        for i in range(1, T):
            pltpu.make_async_remote_copy(
                src_ref=sums_out, dst_ref=sums.at[mine_sum, :], send_sem=sum_sent, recv_sem=sum_sem,
                device_id=(f, tp_peer(t, i)), device_id_type=MESH,
            ).start()

        def send_blocks(b, carry):
            send_block(b)
            return carry

        for a in range(3):
            if a > 0:
                loads[a].wait()
            lax.fori_loop(max(2, 1 + a * PER), 1 + (a + 1) * PER, send_blocks, 0)

    with scope("slots"):
        target_load.wait()
        mine = jnp.concatenate([targets[pl.ds(2 * f, 1), :], targets[pl.ds(2 * f + 1, 1), :]], axis=1).astype(F32)
        across = jnp.broadcast_to(mine, (ROWS, ROWS))
        slot = jnp.sum(jnp.where(across.T < across, 1.0, 0.0), axis=0, keepdims=True)
        line = lax.broadcasted_iota(I32, (SLOTS, 1), 0)
        slot_line = line // 8 * 4 + line % 4
        for h in range(2):
            key = jnp.where(line // 4 % 2 == h, slot_line, -1).astype(F32)
            to_slot[h] = jnp.where(key == slot, 1.0, 0.0).astype(BF16)

    with scope("barrier2"):
        pl.semaphore_wait(x_sem, N_X - 1)
        for dz in range(1, N_Z):
            signal(z_sem, (fsdp_peer(f, 0, 0, dz), t))
    with scope("own"):
        for copy in own:
            copy.wait()
    with scope("waitsum"):
        some = sums.at[pl.ds(0, 8 * (T - 1)), :]
        pltpu.make_async_copy(some, some, sum_sem).wait()
        row_sum[...] = jnp.broadcast_to(jnp.sum(sums[...], axis=0, keepdims=True), (8, LANES))
        row_sums[pl.ds(pl.multiple_of(8 * f, 8), 8), :] = row_sum[...]
    with scope("barrier3"):
        pl.semaphore_wait(z_sem, N_Z - 1)

    others = ROWS - PIECE

    def send(b, dy, dx, dz):
        other = fsdp_peer(f, dy, dx, dz)
        half = b % 2 * 4
        pltpu.make_async_remote_copy(
            src_ref=leaving.at[b, pl.ds(pl.multiple_of(8 * other + half, 4), 4), :],
            dst_ref=arrived.at[b // 2, pl.ds(pl.multiple_of(8 * f + half, 4), 4), :],
            send_sem=fsdp_sent, recv_sem=fsdp_sem.at[b],
            device_id=(other, t), device_id_type=MESH,
        ).start()

    def keep(b):
        half = b % 2 * 4
        arrived[b // 2, pl.ds(pl.multiple_of(8 * f + half, 4), 4), :] = (
            leaving[b, pl.ds(pl.multiple_of(8 * f + half, 4), 4), :])

    def send_all(b):
        def send_line(dy, carry):
            for dx in range(N_X):
                for dz in range(N_Z):
                    send(b, dy, dx, dz)
            return carry

        lax.fori_loop(1, N_Y, send_line, 0)
        for dx in range(N_X):
            for dz in range(N_Z):
                if dx or dz:
                    send(b, 0, dx, dz)

    def send_row_sum(i, carry):
        other = fsdp_peer(f, i // (N_X * N_Z), i // N_Z % N_X, i % N_Z)
        pltpu.make_async_remote_copy(
            src_ref=row_sum.at[pl.ds(0, 1), :],
            dst_ref=row_sums.at[pl.ds(pl.multiple_of(8 * f, 8), 1), :],
            send_sem=row_sent, recv_sem=row_sem,
            device_id=(other, t), device_id_type=MESH,
        ).start()
        return carry

    with scope("issueS"):
        lax.fori_loop(1, F, send_row_sum, 0)

    def send_step(b, carry):
        with scope("waitA"):
            part = whole.at[b, pl.ds(0, others), :]
            pltpu.make_async_copy(part, part, tp_sem.at[b]).wait()
        leaving[b] = moved(to_slot[b % 2], whole[b])
        keep(b)

        with scope("issueB"):
            send_all(b)

        @pl.when(b == 2)
        def _():
            with scope("rows"):
                def widen(s, carry):
                    at = pl.ds(pl.multiple_of(8 * s, 8), 8)
                    wide[at, :LANES] = jnp.broadcast_to(targets[pl.ds(2 * s, 1), :], (8, LANES))
                    wide[at, LANES:] = jnp.broadcast_to(targets[pl.ds(2 * s + 1, 1), :], (8, LANES))
                    return carry

                lax.fori_loop(0, F, widen, 0)
                left = jnp.where(wide[...] // ROWS == f, wide[...] % ROWS, 4096).astype(F32)
                nth = lax.broadcasted_iota(I32, (SLOTS, 1), 0)
                row = jnp.zeros((SLOTS, 1), F32)
                for n in range(4):
                    least = jnp.min(left, axis=1, keepdims=True)
                    row = jnp.where(nth % 4 == n, least, row)
                    if n < 3:
                        left = jnp.where(left == least, 4096.0, left)
                row_key = row + (nth // 4 % 2 * 1024).astype(F32)
                lanes = lax.broadcasted_iota(I32, (SLOTS, SLOTS), 1)
                lane_key = (lanes % ROWS + lanes // ROWS * 1024).astype(F32)
                to_row[...] = jnp.where(row_key == lane_key, 1.0, 0.0).T.astype(BF16)

        return carry

    lax.fori_loop(1, BLOCKS, send_step, 0)

    def put(b, value):
        at = pl.ds(pl.multiple_of((b - 1) % PER * LANES, LANES), LANES)
        out[(b - 1) // PER, :, at] = value

    def place_unit(u, carry):
        with scope("waitB"):
            part = arrived.at[0, pl.ds(0, (SLOTS - 8) // 2), :]

            @pl.when(u > 0)
            def _():
                pltpu.make_async_copy(part, part, fsdp_sem.at[2 * u]).wait()

            pltpu.make_async_copy(part, part, fsdp_sem.at[2 * u + 1]).wait()
        both = moved(to_row[...], arrived[u])

        @pl.when(u > 0)
        def _():
            put(2 * u, both[:ROWS])

        put(2 * u + 1, both[ROWS:])
        return carry

    with scope("clip"):
        some = row_sums.at[pl.ds(0, F - 1), :]
        pltpu.make_async_copy(some, some, row_sem).wait()
        first_line = lax.broadcasted_iota(I32, (SLOTS, LANES), 0) % 8 == 0
        total = jnp.sum(jnp.where(first_line, row_sums[...], 0.0), axis=0, keepdims=True)
        total = jnp.sum(total, axis=1, keepdims=True)
        scale = jnp.minimum(1.0, LIMIT / jnp.sqrt(total))
        clipped[...] = scale * grad[...].astype(F32)

    lax.fori_loop(0, BLOCKS // 2, place_unit, 0)

    with scope("sent"):
        some = sums.at[pl.ds(0, 8 * (T - 1)), :]
        pltpu.make_async_copy(some, some, sum_sent).wait()
        sent = whole.at[pl.ds(1, BLOCKS - 1), pl.ds(0, others), :]
        pltpu.make_async_copy(sent, sent, tp_sent).wait()
        sent = leaving.at[pl.ds(1, BLOCKS - 1), pl.ds(0, (SLOTS - 8) // 2), :]
        pltpu.make_async_copy(sent, sent, fsdp_sent).wait()
        some = row_sums.at[pl.ds(0, F - 1), :]
        pltpu.make_async_copy(some, some, row_sent).wait()


def restore(saved_master, saved_first, saved_second, grad, targets):
    hbm = pl.BlockSpec(memory_space=pltpu.HBM)
    vmem = pl.BlockSpec(memory_space=pltpu.VMEM)
    given = (saved_master, saved_first, saved_second, grad, targets)
    dma = pltpu.SemaphoreType.DMA
    regular = pltpu.SemaphoreType.REGULAR
    return pl.pallas_call(
        kernel,
        out_shape=(
            jax.ShapeDtypeStruct((3, ROWS, COLS), F32),
            jax.ShapeDtypeStruct((ROWS, COLS), F32),
        ),
        in_specs=[hbm] * 5,
        out_specs=(vmem, vmem),
        scratch_shapes=[
            pltpu.VMEM((3, PIECE, D), F32),
            pltpu.VMEM((ROWS, COLS), BF16),
            pltpu.VMEM((H // LANES, LANES), I32),
            pltpu.VMEM((BLOCKS, ROWS, LANES), F32),
            pltpu.VMEM((BLOCKS, SLOTS, LANES), F32),
            pltpu.VMEM((BLOCKS // 2, SLOTS, LANES), F32),
            pltpu.VMEM((8, LANES), F32),
            pltpu.VMEM((8 * T, LANES), F32),
            pltpu.VMEM((8, LANES), F32),
            pltpu.VMEM((SLOTS, LANES), F32),
            pltpu.VMEM((SLOTS, 2 * LANES), I32),
            pltpu.VMEM((2, SLOTS, ROWS), BF16),
            pltpu.VMEM((SLOTS, SLOTS), BF16),
            dma((5,)),
            dma((BLOCKS,)),
            dma,
            dma((BLOCKS,)),
            dma,
            dma((BLOCKS,)),
            dma,
            dma,
            dma,
            dma,
            regular,
            regular,
        ],
        name="restore",
        compiler_params=pltpu.CompilerParams(
            collective_id=0, has_side_effects=True, vmem_limit_bytes=32 * 1024 * 1024
        ),
    )(*(pltpu.with_memory_space_constraint(x, pltpu.HBM) for x in given))


def adam_update(master, first, second, clipped, step):
    first_new = beta_one * first + (1.0 - beta_one) * clipped
    second_new = beta_two * second + (1.0 - beta_two) * clipped * clipped
    count = step[0].astype(jnp.float32)
    first_hat = first_new / (1.0 - jnp.power(jnp.float32(beta_one), count))
    second_hat = second_new / (1.0 - jnp.power(jnp.float32(beta_two), count))
    direction = first_hat / (jnp.sqrt(second_hat) + epsilon) + weight_decay * master
    return (master - learn_rate * direction, first_new, second_new, direction)


def per_device(saved_master, saved_first, saved_second, grad, row_target, step):
    targets = row_target.reshape(H // LANES, LANES)
    state, clipped = restore(saved_master, saved_first, saved_second, grad, targets)
    return adam_update(state[0], state[1], state[2], clipped, step)


def solution(mesh):
    in_specs = (
        P(("fsdp", "tp"), None),
        P(("fsdp", "tp"), None),
        P(("fsdp", "tp"), None),
        P("fsdp", "tp"),
        P(),
        P(),
    )
    out_specs = (P("fsdp", "tp"), P("fsdp", "tp"), P("fsdp", "tp"), P("fsdp", "tp"))
    return jax.shard_map(
        per_device, mesh=mesh, in_specs=in_specs, out_specs=out_specs, check_vma=False
    )
```

time: 177 us -> 88.5 us (0.50)
  the two profiles are of different devices: /device:TPU:8 before, /device:TPU:1 now
where the time goes in v2:
time: 88.5 us; the launch traced here: 88.4 us
  Pallas kernels  85.2 us (96%)
  other arithmetic  1.78 us (2%)
  between operations  1.37 us (2%)
    pallas_call x1, Pallas kernels, restore(): pl.pallas_call(kernel, out_shape=(jax.ShapeDtypeStruct((3, ROWS, COLS), F...  85.2 us
    sub x1, other arithmetic, adam_update(): return (master - learn_rate * direction, first_new, second_new, direction)  1.78 us

profile of v2, /device:TPU:1, one launch (start us, length us, event | category | flops | bytes accessed | tf_op | source)
XLA Modules:
  0.0 88.4 jit_solution(18343042414625459060)
XLA Ops:
  1.4 85.2 %restore.1 = (f32[3,256,640]{2,1,0:T(8,128)S(1)}, f32[256,640]{1,0:T(8,128)S(1)}) custom-call(f32[32,5120]{1,0:T(8,128)} %master.1, f32[32,5120]{1,0:T(8,128)} %first.1, f32[32,5120]{1,0:T(8,128)} %second.1, bf16[256,640]{1,0:T(8,128)(2,1)} %grad_in.1, s32[128,128]{1,0:T(8,128)} %bitcast.15), custom_call_target="tpu_custom_call" | custom-call | tf_op jit(solution)/shard_map/restore/pallas_call | solution.py:297
  86.6 1.8 %bitcast_subtract_fusion = (f32[256,640]{1,0:T(8,128)}, f32[256,640]{1,0:T(8,128)}, f32[256,640]{1,0:T(8,128)}, f32[256,640]{1,0:T(8,128)}) fusion(f32[3,256,640]{2,1,0:T(8,128)S(1)} %get-tuple-element.6, f32[]{:T(128)} %bitcast.5, f32[]{:T(128)} %bitcast.3, f32[256,640]{1,0:T(8,128)S(1)} %get-tuple-element.7), kind=kLoop, calls=%fused_computation.3 | loop fusion | flops 2457600 | bytes 5242888 | tf_op jit(solution)/shard_map/sub | solution.py:346

commit v3 on v2

--- a/solution.py
+++ b/solution.py
@@ -181,31 +181,33 @@
         arrived[b // 2, pl.ds(pl.multiple_of(8 * f + half, 4), 4), :] = (
             leaving[b, pl.ds(pl.multiple_of(8 * f + half, 4), 4), :])
 
+    def to_all(send_one):
+        def send_line(i, carry):
+            dy = N_Y // 2 + (i + 1) // 2 * (1 - 2 * (i % 2))
+            for dx in (2, 1, 3, 0):
+                for dz in (1, 0):
+                    send_one(dy, dx, dz)
+            return carry
+
+        lax.fori_loop(0, N_Y - 1, send_line, 0)
+        for dx in (2, 1, 3, 0):
+            for dz in (1, 0):
+                if dx or dz:
+                    send_one(0, dx, dz)
+
     def send_all(b):
-        def send_line(dy, carry):
-            for dx in range(N_X):
-                for dz in range(N_Z):
-                    send(b, dy, dx, dz)
-            return carry
-
-        lax.fori_loop(1, N_Y, send_line, 0)
-        for dx in range(N_X):
-            for dz in range(N_Z):
-                if dx or dz:
-                    send(b, 0, dx, dz)
-
-    def send_row_sum(i, carry):
-        other = fsdp_peer(f, i // (N_X * N_Z), i // N_Z % N_X, i % N_Z)
+        to_all(lambda dy, dx, dz: send(b, dy, dx, dz))
+
+    def send_row_sum(dy, dx, dz):
         pltpu.make_async_remote_copy(
             src_ref=row_sum.at[pl.ds(0, 1), :],
             dst_ref=row_sums.at[pl.ds(pl.multiple_of(8 * f, 8), 1), :],
             send_sem=row_sent, recv_sem=row_sem,
-            device_id=(other, t), device_id_type=MESH,
+            device_id=(fsdp_peer(f, dy, dx, dz), t), device_id_type=MESH,
         ).start()
-        return carry
 
     with scope("issueS"):
-        lax.fori_loop(1, F, send_row_sum, 0)
+        to_all(send_row_sum)
 
     def send_step(b, carry):
         with scope("waitA"):

time: 88.5 us -> 87.8 us (level)
  no operation moved by 1% of the time
where the time goes in v3:
time: 87.8 us; the launch traced here: 87.7 us
  Pallas kernels  84.5 us (96%)
  other arithmetic  1.78 us (2%)
  between operations  1.37 us (2%)
    pallas_call x1, Pallas kernels, restore(): pl.pallas_call(kernel, out_shape=(jax.ShapeDtypeStruct((3, ROWS, COLS), F...  84.5 us
    sub x1, other arithmetic, adam_update(): return (master - learn_rate * direction, first_new, second_new, direction)  1.78 us

profile of v3, /device:TPU:1, one launch (start us, length us, event | category | flops | bytes accessed | tf_op | source)
XLA Modules:
  0.0 87.7 jit_solution(7395114677668052574)
XLA Ops:
  1.4 84.5 %restore.1 = (f32[3,256,640]{2,1,0:T(8,128)S(1)}, f32[256,640]{1,0:T(8,128)S(1)}) custom-call(f32[32,5120]{1,0:T(8,128)} %master.1, f32[32,5120]{1,0:T(8,128)} %first.1, f32[32,5120]{1,0:T(8,128)} %second.1, bf16[256,640]{1,0:T(8,128)(2,1)} %grad_in.1, s32[128,128]{1,0:T(8,128)} %bitcast.15), custom_call_target="tpu_custom_call" | custom-call | tf_op jit(solution)/shard_map/restore/pallas_call | solution.py:299
  85.9 1.8 %bitcast_subtract_fusion = (f32[256,640]{1,0:T(8,128)}, f32[256,640]{1,0:T(8,128)}, f32[256,640]{1,0:T(8,128)}, f32[256,640]{1,0:T(8,128)}) fusion(f32[3,256,640]{2,1,0:T(8,128)S(1)} %get-tuple-element.6, f32[]{:T(128)} %bitcast.5, f32[]{:T(128)} %bitcast.3, f32[256,640]{1,0:T(8,128)S(1)} %get-tuple-element.7), kind=kLoop, calls=%fused_computation.3 | loop fusion | flops 2457600 | bytes 5242888 | tf_op jit(solution)/shard_map/sub | solution.py:348
